TPU v7x, 32 devices: a whole 2x2x4 slice. The times are simulated.
32 devices in a mesh: grp: 2 (over y), sp: 16 (over z, x, core).
Axes of the slice: x: 2, y: 2, z: 4, core: 2. Of those that a mesh axis runs over, the one named last changes fastest.
Arguments:
- alpha: float32 [20, 16, 4096], P('grp', None, 'sp'), may hold values from -6 to 6
- ensemble: bfloat16 [20, 3, 16, 4096], P('grp', None, None, 'sp'), may hold values from -6 to 6
- static_std: float32 [3, 16, 4096], P(None, 'grp', 'sp'), may hold values from 0.2 to 1
- control: float32 [3, 16, 4096], P(None, 'grp', 'sp'), may hold values from -6 to 6
- loc_spectrum: float32 [1024], replicated, may hold values from 0.00024414062 to 0.001953125
- obs_cell: int32 [32768], P(('grp', 'sp')), may hold values from 0 to 65535, as said below
- obs_step: int32 [32768], P(('grp', 'sp')), may hold values from 0 to 2
- innovation: float32 [32768], P(('grp', 'sp')), may hold values from -6 to 6
- obs_weight: float32 [32768], P(('grp', 'sp')), may hold values from 0.5 to 4
Outputs:
- grad_alpha: float32 [20, 16, 4096], P('grp', None, 'sp')
- grad_control: float32 [3, 16, 4096], P(None, 'grp', 'sp')
Inputs may be any that keep to these rules, and one draw needn't show every extreme that they name: `obs_cell`: an entry is row * 4096 + column. Entries 1024 * b to 1024 * (b + 1) - 1 lie in the tile of 8 rows from row 8 * (b // 16) and 256 columns from column 256 * (b % 16).
All inputs are finite; a program needn't handle non-finite values.
Results may differ from a plain program's by a relative error of at most 0.0075.
Values may be sent and summed in bfloat16 or wider, within the bound.
A program may use at most 128 MiB of HBM per device.

v0:
```python
import math
import jax
import jax.numpy as jnp
import numpy as np
from jax import lax
from jax.sharding import PartitionSpec as P

COURANT = 0.4


def tables(parts, cols, waves):
    length = parts * cols
    inner_waves = waves // parts
    k1 = np.arange(parts)
    turn = 2 * np.pi * (np.outer(k1, np.arange(parts)) % parts) / parts
    outer = np.concatenate([np.cos(turn), -np.sin(turn)])
    twist = 2 * np.pi * np.outer(k1, np.arange(cols)) / length
    phase = 2 * np.pi * (np.outer(np.arange(cols), np.arange(inner_waves)) % cols) / cols
    c, s = (np.cos(phase), np.sin(phase))
    inner = np.block([[c, -s], [s, c]])
    return [np.asarray(t, np.float32) for t in (outer, np.cos(twist), np.sin(twist), inner)]


def mul(a, b):
    return jnp.dot(a, b, precision=lax.Precision.HIGH, preferred_element_type=jnp.float32)


def spectral_filter(blocks, loc_spectrum):
    parts, items, cols = blocks.shape
    outer, tw_c, tw_s, inner = tables(parts, cols, loc_spectrum.shape[0])
    tw_c, tw_s = (tw_c[:, None, :], tw_s[:, None, :])
    half = inner.shape[1] // 2
    weights = loc_spectrum.reshape(half, parts).T
    weights = jnp.concatenate([weights, weights], axis=1)[:, None, :]
    big = np.kron(outer, np.eye(items, dtype=np.float32))
    y = mul(big, blocks.astype(jnp.float32).reshape(parts * items, cols))
    y = y.reshape(2, parts, items, cols)
    y = jnp.concatenate([y[0] * tw_c + y[1] * tw_s, y[1] * tw_c - y[0] * tw_s], axis=2)
    z = mul(y.reshape(parts * items, 2 * cols), inner)
    z = (z.reshape(parts, items, 2 * half) * weights).reshape(parts * items, 2 * half)
    v = mul(z, inner.T).reshape(parts, items, 2, cols)
    re, im = (v[:, :, 0], v[:, :, 1])
    v = jnp.stack([re * tw_c - im * tw_s, im * tw_c + re * tw_s])
    return mul(big.T, v.reshape(2 * parts * items, cols)).reshape(parts, items, cols)


def dx(q):
    return 0.5 * (jnp.roll(q, -1, axis=-1) - jnp.roll(q, 1, axis=-1))


def dy(q):
    padded = jnp.pad(q, ((1, 1), (0, 0)))
    return 0.5 * (padded[2:] - padded[:-2])


def model_step(state, rotation):
    h, u, w = state
    h = h - COURANT * (dx(u) + dy(w))
    return (h, u - COURANT * dx(h) + rotation * w, w - COURANT * dy(h) - rotation * u)


def adjoint_step(state, rotation):
    h, u, w = state
    a = h + COURANT * (dx(u) + dy(w))
    return (a, u - rotation * w + COURANT * dx(a), w + rotation * u + COURANT * dy(a))


HALO = 8


def widen(block):
    count = lax.axis_size("sp")
    up = [(i, (i + 1) % count) for i in range(count)]
    down = [(b, a) for a, b in up]
    low = lax.ppermute(block[..., -HALO:], "sp", up)
    high = lax.ppermute(block[..., :HALO], "sp", down)
    return jnp.concatenate([low, block, high], axis=-1)


def split2(x):
    hi = x.astype(jnp.bfloat16)
    return (hi, (x - hi.astype(jnp.float32)).astype(jnp.bfloat16))


def per_device(
    alpha, ensemble, static_std, control, loc_spectrum, obs_cell, obs_step, innovation, obs_weight
):
    members, rows, cols = alpha.shape
    groups, parts = (lax.axis_size("grp"), lax.axis_size("sp"))
    spread = 1.0 / math.sqrt(members * groups - 1)
    tile_rows = control.shape[1]
    own = rows // parts
    first_row = lax.axis_index("grp") * tile_rows
    first_col = lax.axis_index("sp") * cols

    def localize(fields):
        sent = fields.astype(jnp.bfloat16).transpose(1, 0, 2)
        got = lax.all_to_all(sent, "sp", 0, 0, tiled=True)
        out = spectral_filter(got.reshape(parts, own * members, cols), loc_spectrum)
        out = out.astype(jnp.bfloat16).reshape(rows, members, cols)
        return lax.all_to_all(out, "sp", 0, 0, tiled=True).transpose(1, 0, 2)

    localized = localize(alpha).astype(jnp.float32)
    partial = jnp.sum(ensemble.astype(jnp.float32) * localized[:, None], axis=0)
    base = jnp.zeros((3, rows, cols), jnp.float32)
    base = lax.dynamic_update_slice(base, static_std * control, (0, first_row, 0))
    increment = lax.psum(base + spread * partial, "grp")
    rotation = (0.1 + 0.2 * (jnp.arange(rows, dtype=jnp.float32) + 0.5) / rows)[:, None]
    state0 = tuple(widen(increment))
    state1 = model_step(state0, rotation)
    state2 = model_step(state1, rotation)
    heights = jnp.stack([s[0] for s in (state0, state1, state2)])[..., HALO:-HALO]
    heights = lax.dynamic_slice_in_dim(heights, first_row, tile_rows, axis=1)
    heights = heights.reshape(3 * tile_rows, cols)
    row = obs_cell // (cols * parts) - first_row
    col = obs_cell % (cols * parts) - first_col
    in_col = (col[:, None] == jnp.arange(cols)).astype(jnp.bfloat16)
    in_row = (obs_step * tile_rows + row)[:, None] == jnp.arange(3 * tile_rows)
    picked = jnp.dot(in_col, jnp.concatenate(split2(heights)).T, preferred_element_type=jnp.float32)
    picked = picked[:, : 3 * tile_rows] + picked[:, 3 * tile_rows :]
    observed = jnp.sum(jnp.where(in_row, picked, 0.0), axis=1)
    misfit = obs_weight * (observed - innovation)
    placed = jnp.where(in_row, misfit[:, None], 0.0)
    forcing = jnp.dot(
        jnp.concatenate(split2(placed), axis=1).T, in_col, preferred_element_type=jnp.float32
    )
    forcing = (forcing[: 3 * tile_rows] + forcing[3 * tile_rows :]).reshape(3, tile_rows, cols)
    forcing = widen(lax.all_gather(forcing, "grp", axis=1, tiled=True))
    zero = jnp.zeros_like(forcing[0])
    h, u, w = adjoint_step((forcing[2], zero, zero), rotation)
    h, u, w = adjoint_step((h + forcing[1], u, w), rotation)
    adjoint = jnp.stack([h + forcing[0], u, w])[..., HALO:-HALO]
    tile = lax.dynamic_slice_in_dim(adjoint, first_row, tile_rows, axis=1)
    grad_control = control + static_std * tile
    half = adjoint.astype(jnp.bfloat16).astype(jnp.float32)
    weighted = jnp.sum(ensemble.astype(jnp.float32) * half[None], axis=1)
    grad_alpha = alpha + spread * localize(weighted).astype(jnp.float32)
    return (grad_alpha, grad_control)


def solution(mesh):
    flat = P(("grp", "sp"))
    tile = P(None, "grp", "sp")
    return jax.shard_map(
        per_device,
        mesh=mesh,
        in_specs=(
            P("grp", None, "sp"),
            P("grp", None, None, "sp"),
            tile,
            tile,
            P(),
            flat,
            flat,
            flat,
            flat,
        ),
        out_specs=(P("grp", None, "sp"), tile),
        check_vma=False,
    )
```

profile of v0, /device:TPU:0, one launch (start us, length us, event | category | flops | bytes accessed | tf_op | source)
XLA Modules:
  0.0 93.3 jit_solution(1954184808317779153)
XLA Ops:
  0.6 0.9 convert_bitcast_fusion.2
  1.6 0.7 copy.66
  2.3 7.5 %all-to-all-start = ((bf16[16,10,256]{2,1,0:T(8,128)(2,1)}), bf16[16,10,256]{2,1,0:T(8,128)(2,1)S(1)}, u32[]{:S(2)}, u32[]{:S(2)}) async-start(bf16[16,10,256]{2,1,0:T(8,128)(2,1)} %copy.66), calls=%async_computation | async-start | bytes 262144 | tf_op jit(solution)/shard_map/all_to_all | solution.py:98
  9.8 0.7 copy-done.7
  10.6 0.7 copy-done.8
  11.3 0.6 copy-done.13
  12.1 0.1 pad_maximum_fusion.6
  12.2 5.5 %all-to-all-done = bf16[16,10,256]{2,1,0:T(8,128)(2,1)S(1)} async-done(((bf16[16,10,256]{2,1,0:T(8,128)(2,1)}), bf16[16,10,256]{2,1,0:T(8,128)(2,1)S(1)}, u32[]{:S(2)}, u32[]{:S(2)}) %all-to-all-start) | async-done | bytes 81952 | tf_op jit(solution)/shard_map/all_to_all | solution.py:98
  17.7 0.2 fusion.94
  18.1 0.9 copy-done.1
  19.0 0.4 fusion
  19.4 0.6 copy-done.6
  20.0 0.3 fusion.23
  20.4 0.2 copy.71
  20.6 0.9 copy-done.3
  21.5 0.3 fusion.1
  21.8 0.7 convert_element_type.81
  22.5 3.5 %all-to-all-start.1 = ((bf16[16,10,256]{2,1,0:T(8,128)(2,1)}), bf16[16,10,256]{2,1,0:T(8,128)(2,1)S(1)}, u32[]{:S(2)}, u32[]{:S(2)}) async-start(bf16[16,10,256]{2,1,0:T(8,128)(2,1)} %convert_element_type.81), calls=%async_computation.1 | async-start | bytes 262144 | tf_op jit(solution)/shard_map/all_to_all | solution.py:101
  26.0 7.8 %all-to-all-done.1 = bf16[16,10,256]{2,1,0:T(8,128)(2,1)S(1)} async-done(((bf16[16,10,256]{2,1,0:T(8,128)(2,1)}), bf16[16,10,256]{2,1,0:T(8,128)(2,1)S(1)}, u32[]{:S(2)}, u32[]{:S(2)}) %all-to-all-start.1) | async-done | bytes 81952 | tf_op jit(solution)/shard_map/all_to_all | solution.py:101
  33.9 0.1 copy.72
  34.0 0.8 copy-done.2
  34.9 0.7 copy-done.9
  35.7 8.6 %psum.7 = f32[3,16,256]{2,1,0:T(8,128)S(1)} all-reduce(f32[3,16,256]{2,1,0:T(8,128)S(1)} %add_dynamic-update-slice_fusion), channel_id=1, replica_groups=mesh['grp'=2,'sp'=16] {'grp'}, use_global_device_ids=true, to_apply=%region_1.0 | all-reduce | flops 12288 | bytes 98304 | tf_op jit(solution)/shard_map/psum | solution.py:107
  44.3 0.1 fusion.81
  44.4 4.4 %collective-permute-start.1 = (f32[3,16,8]{2,1,0:T(8,128)S(1)}, f32[3,16,8]{2,1,0:T(8,128)S(1)}, u32[]{:S(2)}, u32[]{:S(2)}) collective-permute-start(f32[3,16,8]{2,1,0:T(8,128)S(1)} %get-tuple-element.34), channel_id=1, source_target_pairs={{1,0},{2,1},{3,2},{4,3},{5,4},{6,5},{7,6},{8,7},{9,8},{10,9},{11,1... | collective-permute-start | bytes 4616 | tf_op jit(solution)/shard_map/ppermute | solution.py:76
  48.9 1.5 %collective-permute-done = f32[3,16,8]{2,1,0:T(8,128)S(1)} collective-permute-done((f32[3,16,8]{2,1,0:T(8,128)S(1)}, f32[3,16,8]{2,1,0:T(8,128)S(1)}, u32[]{:S(2)}, u32[]{:S(2)}) %collective-permute-start) | collective-permute-done | bytes 1568 | tf_op jit(solution)/shard_map/ppermute | solution.py:75
  50.4 0.1 pad_maximum_fusion.2
  50.5 0.1 fusion.93
  50.6 0.1 fusion.29
  50.7 0.1 fusion.91
  50.9 0.1 fusion.60
  50.9 0.1 fusion.89
  51.1 0.1 fusion.38
  51.2 0.1 subtract_convert_fusion
  51.3 0.4 fusion.4
  51.7 0.6 copy-done.14
  52.4 0.4 fusion.3
  52.8 4.5 %all_gather.3 = f32[3,16,256]{2,1,0:T(8,128)S(1)} all-gather(f32[3,8,256]{2,1,0:T(8,128)S(1)} %fusion.57), channel_id=1, replica_groups=mesh['grp'=2,'sp'=16] {'grp'}, dimensions={1}, use_global_device_ids=true | all-gather | bytes 73728 | tf_op jit(solution)/shard_map/all_gather | solution.py:128
  57.3 0.1 fusion.80
  57.3 4.4 %collective-permute-start.3 = (f32[3,16,8]{2,1,0:T(8,128)S(1)}, f32[3,16,8]{2,1,0:T(8,128)S(1)}, u32[]{:S(2)}, u32[]{:S(2)}) collective-permute-start(f32[3,16,8]{2,1,0:T(8,128)S(1)} %get-tuple-element.32), channel_id=1, source_target_pairs={{1,0},{2,1},{3,2},{4,3},{5,4},{6,5},{7,6},{8,7},{9,8},{10,9},{11,1... | collective-permute-start | bytes 4616 | tf_op jit(solution)/shard_map/ppermute | solution.py:76
  61.8 0.1 fusion.74
  61.9 1.4 %collective-permute-done.2 = f32[3,16,8]{2,1,0:T(8,128)S(1)} collective-permute-done((f32[3,16,8]{2,1,0:T(8,128)S(1)}, f32[3,16,8]{2,1,0:T(8,128)S(1)}, u32[]{:S(2)}, u32[]{:S(2)}) %collective-permute-start.2) | collective-permute-done | bytes 1568 | tf_op jit(solution)/shard_map/ppermute | solution.py:75
  63.3 0.1 pad_maximum_fusion.3
  63.4 0.1 fusion.56
  63.5 0.1 fusion.87
  63.6 0.1 fusion.41
  63.7 0.1 fusion.84
  63.9 0.1 fusion.54
  64.0 0.1 fusion.83
  64.1 0.1 fusion.68
  64.2 0.1 convert_convert_fusion
  64.4 13.5 %all_to_all.20 = bf16[16,10,256]{2,1,0:T(8,128)(2,1)S(1)} all-to-all(bf16[16,10,256]{2,1,0:T(8,128)(2,1)S(1)} %copy.73), channel_id=1, replica_groups=mesh['grp'=2,'sp'=16] {'sp'}, dimensions={0} | all-to-all | bytes 163840 | tf_op jit(solution)/shard_map/all_to_all | solution.py:98
  77.9 0.2 fusion.95
  78.3 0.4 convolution_multiply_fusion
  78.7 0.5 copy-done.5
  79.2 0.3 fusion.21
  79.6 0.2 copy.77
  79.9 0.3 fusion.2
  80.2 0.7 convert_element_type.96
  80.9 3.6 %all-to-all-start.3 = ((bf16[16,10,256]{2,1,0:T(8,128)(2,1)}), bf16[16,10,256]{2,1,0:T(8,128)(2,1)S(1)}, u32[]{:S(2)}, u32[]{:S(2)}) async-start(bf16[16,10,256]{2,1,0:T(8,128)(2,1)} %convert_element_type.96), calls=%async_computation.3 | async-start | bytes 262144 | tf_op jit(solution)/shard_map/all_to_all | solution.py:101
  84.5 0.6 multiply_add_fusion.4
  85.1 7.2 %all-to-all-done.3 = bf16[16,10,256]{2,1,0:T(8,128)(2,1)S(1)} async-done(((bf16[16,10,256]{2,1,0:T(8,128)(2,1)}), bf16[16,10,256]{2,1,0:T(8,128)(2,1)S(1)}, u32[]{:S(2)}, u32[]{:S(2)}) %all-to-all-start.3) | async-done | bytes 81952 | tf_op jit(solution)/shard_map/all_to_all | solution.py:101
  92.4 0.1 bitcast_add_fusion
  92.5 0.8 copy.79
  (71 shorter events, 1.6 us)
Async XLA Ops:
  2.2 7.5 %copy-start.11 = (s32[1024]{0:T(1024)S(1)}, s32[1024]{0:T(1024)}, u32[]{:S(2)}) copy-start(s32[1024]{0:T(1024)} %param.27) | copy-start | bytes 12292
  2.2 7.6 %copy-start.12 = (s32[1024]{0:T(1024)S(1)}, s32[1024]{0:T(1024)}, u32[]{:S(2)}) copy-start(s32[1024]{0:T(1024)} %param.26) | copy-start | bytes 12292
  2.3 15.4 %all-to-all-start = ((bf16[16,10,256]{2,1,0:T(8,128)(2,1)}), bf16[16,10,256]{2,1,0:T(8,128)(2,1)S(1)}, u32[]{:S(2)}, u32[]{:S(2)}) async-start(bf16[16,10,256]{2,1,0:T(8,128)(2,1)} %copy.66), calls=%async_computation | async-start | bytes 262144 | tf_op jit(solution)/shard_map/all_to_all | solution.py:98
  9.8 0.7 copy-start.7
  10.5 0.7 copy-start.8
  11.3 0.7 copy-start.13
  11.3 6.4 %copy-start = (f32[320,160]{1,0:T(8,128)S(1)}, f32[320,160]{1,0:T(8,128)}, u32[]{:S(2)}) copy-start(f32[320,160]{1,0:T(8,128)} %constant.90.clone) | copy-start | bytes 614404
  18.1 1.0 %copy-start.1 = (f32[512,128,1]{1,0,2:T(8,128)S(1)}, f32[512,128,1]{1,0,2:T(8,128)}, u32[]{:S(2)}) copy-start(f32[512,128,1]{1,0,2:T(8,128)} %constant.116) | copy-start | bytes 786436
  19.0 0.9 %copy-start.6 = (f32[2,256,128,1]{2,1,0,3:T(8,128)S(1)}, f32[2,256,128,1]{2,1,0,3:T(8,128)}, u32[]{:S(2)}) copy-start(f32[2,256,128,1]{2,1,0,3:T(8,128)} %constant.117) | copy-start | bytes 786436
  20.6 0.9 %copy-start.3 = (f32[160,320]{1,0:T(8,128)S(1)}, f32[160,320]{1,0:T(8,128)}, u32[]{:S(2)}) copy-start(f32[160,320]{1,0:T(8,128)} %constant.95.clone) | copy-start | bytes 614404
  22.5 11.4 %all-to-all-start.1 = ((bf16[16,10,256]{2,1,0:T(8,128)(2,1)}), bf16[16,10,256]{2,1,0:T(8,128)(2,1)S(1)}, u32[]{:S(2)}, u32[]{:S(2)}) async-start(bf16[16,10,256]{2,1,0:T(8,128)(2,1)} %convert_element_type.81), calls=%async_computation.1 | async-start | bytes 262144 | tf_op jit(solution)/shard_map/all_to_all | solution.py:101
  33.9 0.9 %copy-start.2 = (bf16[10,3,16,256]{3,2,1,0:T(8,128)(2,1)S(1)}, bf16[10,3,16,256]{3,2,1,0:T(8,128)(2,1)}, u32[]{:S(2)}) copy-start(bf16[10,3,16,256]{3,2,1,0:T(8,128)(2,1)} %param.22) | copy-start | bytes 737284
  34.9 0.7 copy-start.9
  34.9 0.7 copy-start.10
  44.4 6.0 %collective-permute-start = (f32[3,16,8]{2,1,0:T(8,128)S(1)}, f32[3,16,8]{2,1,0:T(8,128)S(1)}, u32[]{:S(2)}, u32[]{:S(2)}) collective-permute-start(f32[3,16,8]{2,1,0:T(8,128)S(1)} %get-tuple-element.33), channel_id=1, source_target_pairs={{0,1},{1,2},{2,3},{3,4},{4,5},{5,6},{6,7},{7,8},{8,9},{9,10},{10,1... | collective-permute-start | bytes 4616 | tf_op jit(solution)/shard_map/ppermute | solution.py:75
  44.4 6.0 %collective-permute-start.1 = (f32[3,16,8]{2,1,0:T(8,128)S(1)}, f32[3,16,8]{2,1,0:T(8,128)S(1)}, u32[]{:S(2)}, u32[]{:S(2)}) collective-permute-start(f32[3,16,8]{2,1,0:T(8,128)S(1)} %get-tuple-element.34), channel_id=1, source_target_pairs={{1,0},{2,1},{3,2},{4,3},{5,4},{6,5},{7,6},{8,7},{9,8},{10,9},{11,1... | collective-permute-start | bytes 4616 | tf_op jit(solution)/shard_map/ppermute | solution.py:76
  51.6 0.7 copy-start.14
  51.6 0.7 copy-start.15
  57.3 6.0 %collective-permute-start.2 = (f32[3,16,8]{2,1,0:T(8,128)S(1)}, f32[3,16,8]{2,1,0:T(8,128)S(1)}, u32[]{:S(2)}, u32[]{:S(2)}) collective-permute-start(f32[3,16,8]{2,1,0:T(8,128)S(1)} %get-tuple-element.31), channel_id=1, source_target_pairs={{0,1},{1,2},{2,3},{3,4},{4,5},{5,6},{6,7},{7,8},{8,9},{9,10},{10,1... | collective-permute-start | bytes 4616 | tf_op jit(solution)/shard_map/ppermute | solution.py:75
  57.3 6.0 %collective-permute-start.3 = (f32[3,16,8]{2,1,0:T(8,128)S(1)}, f32[3,16,8]{2,1,0:T(8,128)S(1)}, u32[]{:S(2)}, u32[]{:S(2)}) collective-permute-start(f32[3,16,8]{2,1,0:T(8,128)S(1)} %get-tuple-element.32), channel_id=1, source_target_pairs={{1,0},{2,1},{3,2},{4,3},{5,4},{6,5},{7,6},{8,7},{9,8},{10,9},{11,1... | collective-permute-start | bytes 4616 | tf_op jit(solution)/shard_map/ppermute | solution.py:76
  78.3 1.0 %copy-start.5 = (f32[2,256,128,1]{2,1,3,0:T(8,128)S(1)}, f32[2,256,128,1]{2,1,3,0:T(8,128)}, u32[]{:S(2)}) copy-start(f32[2,256,128,1]{2,1,3,0:T(8,128)} %constant.118) | copy-start | bytes 786436
  80.9 11.5 %copy-start.4 = (f32[10,16,256]{2,1,0:T(8,128)S(1)}, f32[10,16,256]{2,1,0:T(8,128)}, u32[]{:S(2)}) copy-start(f32[10,16,256]{2,1,0:T(8,128)} %param.21) | copy-start | bytes 491524
  80.9 11.5 %all-to-all-start.3 = ((bf16[16,10,256]{2,1,0:T(8,128)(2,1)}), bf16[16,10,256]{2,1,0:T(8,128)(2,1)S(1)}, u32[]{:S(2)}, u32[]{:S(2)}) async-start(bf16[16,10,256]{2,1,0:T(8,128)(2,1)} %convert_element_type.96), calls=%async_computation.3 | async-start | bytes 262144 | tf_op jit(solution)/shard_map/all_to_all | solution.py:101
where the time goes:
time: 94.1 us; the launch traced here: 93.3 us
  blocking collectives  26.7 us (28%)
  starting transfers between devices  23.6 us (25%)
  waiting for transfers between devices  23.5 us (25%)
  local copies, waits for them, and re-layouts  12 us (13%)
  other arithmetic  3.23 us (3%)
  matrix products  3.1 us (3%)
  between operations  1.17 us (1%)
    all_to_all x2, waiting for transfers between devices, localize(): return lax.all_to_all(out, 'sp', 0, 0, tiled=True).transpose(1, 0, 2)  15.1 us
    all_to_all x1, blocking collectives, localize(): got = lax.all_to_all(sent, 'sp', 0, 0, tiled=True)  13.5 us
    ppermute x2, starting transfers between devices, widen(): high = lax.ppermute(block[..., :HALO], 'sp', down)  8.88 us
    psum x1, blocking collectives, per_device(): increment = lax.psum(base + spread * partial, 'grp')  8.65 us
    unnamed x33, local copies, waits for them, and re-layouts  7.9 us
    all_to_all x1, starting transfers between devices, localize(): got = lax.all_to_all(sent, 'sp', 0, 0, tiled=True)  7.52 us
    all_to_all x2, starting transfers between devices, localize(): return lax.all_to_all(out, 'sp', 0, 0, tiled=True).transpose(1, 0, 2)  7.16 us
    all_to_all x1, waiting for transfers between devices, localize(): got = lax.all_to_all(sent, 'sp', 0, 0, tiled=True)  5.51 us
  transfers between devices with their start and end apart: 7, of which 5 were waited for; matrix products, arithmetic and copies ran while one was open for 1% of the time, Pallas kernels for 0%

commit v1 on v0

--- a/solution.py
+++ b/solution.py
@@ -104,7 +104,9 @@
     partial = jnp.sum(ensemble.astype(jnp.float32) * localized[:, None], axis=0)
     base = jnp.zeros((3, rows, cols), jnp.float32)
     base = lax.dynamic_update_slice(base, static_std * control, (0, first_row, 0))
-    increment = lax.psum(base + spread * partial, "grp")
+    block_2 = base + spread * partial
+    pieces = lax.all_gather(block_2, "grp")
+    increment = jnp.sum(pieces, axis=0)
     rotation = (0.1 + 0.2 * (jnp.arange(rows, dtype=jnp.float32) + 0.5) / rows)[:, None]
     state0 = tuple(widen(increment))
     state1 = model_step(state0, rotation)

time: 94.1 us -> 90.2 us (0.959)
  blocking collectives: 26.7 us -> 22.8 us
    psum x1 -> x0, blocking collectives: 8.65 us -> none  [per_device(): increment = lax.psum(base + spread * partial, 'grp')]
    all_gather x0 -> x1, blocking collectives: none -> 4.75 us  [per_device(): pieces = lax.all_gather(block_2, 'grp')]
where the time goes in v1:
time: 90.2 us; the launch traced here: 89.4 us
  starting transfers between devices  23.6 us (26%)
  waiting for transfers between devices  23.5 us (26%)
  blocking collectives  22.8 us (25%)
  local copies, waits for them, and re-layouts  12 us (13%)
  other arithmetic  3.25 us (4%)
  matrix products  3.09 us (3%)
  between operations  1.17 us (1%)
    all_to_all x2, waiting for transfers between devices, localize(): return lax.all_to_all(out, 'sp', 0, 0, tiled=True).transpose(1, 0, 2)  15.1 us
    all_to_all x1, blocking collectives, localize(): got = lax.all_to_all(sent, 'sp', 0, 0, tiled=True)  13.5 us
    ppermute x2, starting transfers between devices, widen(): high = lax.ppermute(block[..., :HALO], 'sp', down)  8.88 us
    unnamed x33, local copies, waits for them, and re-layouts  7.91 us
    all_to_all x1, starting transfers between devices, localize(): got = lax.all_to_all(sent, 'sp', 0, 0, tiled=True)  7.52 us
    all_to_all x2, starting transfers between devices, localize(): return lax.all_to_all(out, 'sp', 0, 0, tiled=True).transpose(1, 0, 2)  7.16 us
    all_to_all x1, waiting for transfers between devices, localize(): got = lax.all_to_all(sent, 'sp', 0, 0, tiled=True)  5.51 us
    all_gather x1, blocking collectives, per_device(): pieces = lax.all_gather(block_2, 'grp')  4.75 us
  transfers between devices with their start and end apart: 7, of which 5 were waited for; matrix products, arithmetic and copies ran while one was open for 1% of the time, Pallas kernels for 0%

profile of v1, /device:TPU:0, one launch (start us, length us, event | category | flops | bytes accessed | tf_op | source)
XLA Modules:
  0.0 89.4 jit_solution(6937438591136755106)
XLA Ops:
  0.6 0.9 %convert_bitcast_fusion.2 = bf16[16,10,256]{2,0,1:T(8,128)(2,1)S(1)} fusion(f32[10,16,256]{2,1,0:T(8,128)} %param.21), kind=kLoop, calls=%fused_computation.54 | loop fusion | flops 40960 | bytes 245760 | tf_op jit(solution)/shard_map/transpose | solution.py:97
  1.6 0.7 copy.66
  2.3 7.5 %all-to-all-start = ((bf16[16,10,256]{2,1,0:T(8,128)(2,1)}), bf16[16,10,256]{2,1,0:T(8,128)(2,1)S(1)}, u32[]{:S(2)}, u32[]{:S(2)}) async-start(bf16[16,10,256]{2,1,0:T(8,128)(2,1)} %copy.66), calls=%async_computation | async-start | bytes 262144 | tf_op jit(solution)/shard_map/all_to_all | solution.py:98
  9.8 0.7 copy-done.7
  10.6 0.7 copy-done.8
  11.3 0.6 copy-done.13
  12.1 0.1 pad_maximum_fusion.6
  12.2 5.5 %all-to-all-done = bf16[16,10,256]{2,1,0:T(8,128)(2,1)S(1)} async-done(((bf16[16,10,256]{2,1,0:T(8,128)(2,1)}), bf16[16,10,256]{2,1,0:T(8,128)(2,1)S(1)}, u32[]{:S(2)}, u32[]{:S(2)}) %all-to-all-start) | async-done | bytes 81952 | tf_op jit(solution)/shard_map/all_to_all | solution.py:98
  17.7 0.2 fusion.95
  18.1 0.9 %copy-done.1 = f32[512,128,1]{1,0,2:T(8,128)S(1)} copy-done((f32[512,128,1]{1,0,2:T(8,128)S(1)}, f32[512,128,1]{1,0,2:T(8,128)}, u32[]{:S(2)}) %copy-start.1) | copy-done | bytes 262168
  19.0 0.4 fusion
  19.4 0.6 copy-done.6
  20.0 0.3 fusion.23
  20.4 0.2 copy.71
  20.6 0.9 copy-done.3
  21.5 0.3 fusion.1
  21.8 0.7 convert_element_type.81
  22.5 3.5 %all-to-all-start.1 = ((bf16[16,10,256]{2,1,0:T(8,128)(2,1)}), bf16[16,10,256]{2,1,0:T(8,128)(2,1)S(1)}, u32[]{:S(2)}, u32[]{:S(2)}) async-start(bf16[16,10,256]{2,1,0:T(8,128)(2,1)} %convert_element_type.81), calls=%async_computation.1 | async-start | bytes 262144 | tf_op jit(solution)/shard_map/all_to_all | solution.py:101
  26.0 7.8 %all-to-all-done.1 = bf16[16,10,256]{2,1,0:T(8,128)(2,1)S(1)} async-done(((bf16[16,10,256]{2,1,0:T(8,128)(2,1)}), bf16[16,10,256]{2,1,0:T(8,128)(2,1)S(1)}, u32[]{:S(2)}, u32[]{:S(2)}) %all-to-all-start.1) | async-done | bytes 81952 | tf_op jit(solution)/shard_map/all_to_all | solution.py:101
  33.9 0.1 copy.72
  34.0 0.8 copy-done.2
  34.9 0.7 copy-done.9
  35.7 4.7 %all_gather.10 = f32[2,3,16,256]{3,2,1,0:T(8,128)S(1)} all-gather(f32[1,3,16,256]{3,2,1,0:T(8,128)S(1)} %bitcast_dynamic-update-slice_fusion), channel_id=1, replica_groups=mesh['grp'=2,'sp'=16] {'grp'}, dimensions={0}, use_global_device_ids=true | all-gather | bytes 147456 | tf_op jit(solution)/shard_map/all_gather | solution.py:108
  40.4 0.1 fusion.82
  40.5 4.4 %collective-permute-start.1 = (f32[3,16,8]{2,1,0:T(8,128)S(1)}, f32[3,16,8]{2,1,0:T(8,128)S(1)}, u32[]{:S(2)}, u32[]{:S(2)}) collective-permute-start(f32[3,16,8]{2,1,0:T(8,128)S(1)} %get-tuple-element.34), channel_id=1, source_target_pairs={{1,0},{2,1},{3,2},{4,3},{5,4},{6,5},{7,6},{8,7},{9,8},{10,9},{11,1... | collective-permute-start | bytes 4616 | tf_op jit(solution)/shard_map/ppermute | solution.py:76
  45.0 1.5 %collective-permute-done = f32[3,16,8]{2,1,0:T(8,128)S(1)} collective-permute-done((f32[3,16,8]{2,1,0:T(8,128)S(1)}, f32[3,16,8]{2,1,0:T(8,128)S(1)}, u32[]{:S(2)}, u32[]{:S(2)}) %collective-permute-start) | collective-permute-done | bytes 1568 | tf_op jit(solution)/shard_map/ppermute | solution.py:75
  46.5 0.1 pad_maximum_fusion.2
  46.6 0.1 fusion.94
  46.7 0.1 fusion.29
  46.8 0.1 fusion.92
  47.0 0.1 fusion.60
  47.1 0.1 fusion.90
  47.2 0.1 fusion.38
  47.3 0.1 subtract_convert_fusion
  47.4 0.4 fusion.4
  47.8 0.6 copy-done.14
  48.5 0.4 fusion.3
  48.9 4.5 %all_gather.11 = f32[3,16,256]{2,1,0:T(8,128)S(1)} all-gather(f32[3,8,256]{2,1,0:T(8,128)S(1)} %fusion.57), channel_id=1, replica_groups=mesh['grp'=2,'sp'=16] {'grp'}, dimensions={1}, use_global_device_ids=true | all-gather | bytes 73728 | tf_op jit(solution)/shard_map/all_gather | solution.py:130
  53.4 0.1 fusion.81
  53.4 4.4 %collective-permute-start.3 = (f32[3,16,8]{2,1,0:T(8,128)S(1)}, f32[3,16,8]{2,1,0:T(8,128)S(1)}, u32[]{:S(2)}, u32[]{:S(2)}) collective-permute-start(f32[3,16,8]{2,1,0:T(8,128)S(1)} %get-tuple-element.32), channel_id=1, source_target_pairs={{1,0},{2,1},{3,2},{4,3},{5,4},{6,5},{7,6},{8,7},{9,8},{10,9},{11,1... | collective-permute-start | bytes 4616 | tf_op jit(solution)/shard_map/ppermute | solution.py:76
  57.9 0.1 fusion.74
  58.0 1.4 %collective-permute-done.2 = f32[3,16,8]{2,1,0:T(8,128)S(1)} collective-permute-done((f32[3,16,8]{2,1,0:T(8,128)S(1)}, f32[3,16,8]{2,1,0:T(8,128)S(1)}, u32[]{:S(2)}, u32[]{:S(2)}) %collective-permute-start.2) | collective-permute-done | bytes 1568 | tf_op jit(solution)/shard_map/ppermute | solution.py:75
  59.4 0.1 pad_maximum_fusion.3
  59.5 0.1 fusion.56
  59.6 0.1 fusion.88
  59.7 0.1 fusion.41
  59.8 0.1 fusion.85
  60.0 0.1 fusion.54
  60.1 0.1 fusion.84
  60.2 0.1 fusion.68
  60.3 0.1 convert_convert_fusion
  60.5 13.5 %all_to_all.20 = bf16[16,10,256]{2,1,0:T(8,128)(2,1)S(1)} all-to-all(bf16[16,10,256]{2,1,0:T(8,128)(2,1)S(1)} %copy.73), channel_id=1, replica_groups=mesh['grp'=2,'sp'=16] {'sp'}, dimensions={0} | all-to-all | bytes 163840 | tf_op jit(solution)/shard_map/all_to_all | solution.py:98
  74.0 0.2 fusion.96
  74.4 0.4 convolution_multiply_fusion
  74.8 0.6 copy-done.5
  75.4 0.3 fusion.21
  75.7 0.2 copy.77
  76.0 0.3 fusion.2
  76.3 0.7 convert_element_type.96
  77.0 3.6 %all-to-all-start.3 = ((bf16[16,10,256]{2,1,0:T(8,128)(2,1)}), bf16[16,10,256]{2,1,0:T(8,128)(2,1)S(1)}, u32[]{:S(2)}, u32[]{:S(2)}) async-start(bf16[16,10,256]{2,1,0:T(8,128)(2,1)} %convert_element_type.96), calls=%async_computation.3 | async-start | bytes 262144 | tf_op jit(solution)/shard_map/all_to_all | solution.py:101
  80.6 0.6 multiply_add_fusion.4
  81.3 7.2 %all-to-all-done.3 = bf16[16,10,256]{2,1,0:T(8,128)(2,1)S(1)} async-done(((bf16[16,10,256]{2,1,0:T(8,128)(2,1)}), bf16[16,10,256]{2,1,0:T(8,128)(2,1)S(1)}, u32[]{:S(2)}, u32[]{:S(2)}) %all-to-all-start.3) | async-done | bytes 81952 | tf_op jit(solution)/shard_map/all_to_all | solution.py:101
  88.5 0.1 bitcast_add_fusion
  88.6 0.8 copy.79
  (72 shorter events, 1.6 us)
Async XLA Ops:
  2.2 7.5 %copy-start.11 = (s32[1024]{0:T(1024)S(1)}, s32[1024]{0:T(1024)}, u32[]{:S(2)}) copy-start(s32[1024]{0:T(1024)} %param.27) | copy-start | bytes 12292
  2.2 7.6 %copy-start.12 = (s32[1024]{0:T(1024)S(1)}, s32[1024]{0:T(1024)}, u32[]{:S(2)}) copy-start(s32[1024]{0:T(1024)} %param.26) | copy-start | bytes 12292
  2.3 15.4 %all-to-all-start = ((bf16[16,10,256]{2,1,0:T(8,128)(2,1)}), bf16[16,10,256]{2,1,0:T(8,128)(2,1)S(1)}, u32[]{:S(2)}, u32[]{:S(2)}) async-start(bf16[16,10,256]{2,1,0:T(8,128)(2,1)} %copy.66), calls=%async_computation | async-start | bytes 262144 | tf_op jit(solution)/shard_map/all_to_all | solution.py:98
  9.8 0.7 copy-start.7
  10.5 0.7 copy-start.8
  11.3 0.7 copy-start.13
  11.3 6.4 %copy-start = (f32[320,160]{1,0:T(8,128)S(1)}, f32[320,160]{1,0:T(8,128)}, u32[]{:S(2)}) copy-start(f32[320,160]{1,0:T(8,128)} %constant.91.clone) | copy-start | bytes 614404
  18.1 1.0 %copy-start.1 = (f32[512,128,1]{1,0,2:T(8,128)S(1)}, f32[512,128,1]{1,0,2:T(8,128)}, u32[]{:S(2)}) copy-start(f32[512,128,1]{1,0,2:T(8,128)} %constant.117) | copy-start | bytes 786436
  19.0 0.9 %copy-start.6 = (f32[2,256,128,1]{2,1,0,3:T(8,128)S(1)}, f32[2,256,128,1]{2,1,0,3:T(8,128)}, u32[]{:S(2)}) copy-start(f32[2,256,128,1]{2,1,0,3:T(8,128)} %constant.118) | copy-start | bytes 786436
  20.6 0.9 %copy-start.3 = (f32[160,320]{1,0:T(8,128)S(1)}, f32[160,320]{1,0:T(8,128)}, u32[]{:S(2)}) copy-start(f32[160,320]{1,0:T(8,128)} %constant.96.clone) | copy-start | bytes 614404
  22.5 11.4 %all-to-all-start.1 = ((bf16[16,10,256]{2,1,0:T(8,128)(2,1)}), bf16[16,10,256]{2,1,0:T(8,128)(2,1)S(1)}, u32[]{:S(2)}, u32[]{:S(2)}) async-start(bf16[16,10,256]{2,1,0:T(8,128)(2,1)} %convert_element_type.81), calls=%async_computation.1 | async-start | bytes 262144 | tf_op jit(solution)/shard_map/all_to_all | solution.py:101
  33.9 0.9 %copy-start.2 = (bf16[10,3,16,256]{3,2,1,0:T(8,128)(2,1)S(1)}, bf16[10,3,16,256]{3,2,1,0:T(8,128)(2,1)}, u32[]{:S(2)}) copy-start(bf16[10,3,16,256]{3,2,1,0:T(8,128)(2,1)} %param.22) | copy-start | bytes 737284
  34.9 0.7 copy-start.9
  34.9 0.7 copy-start.10
  40.5 6.0 %collective-permute-start = (f32[3,16,8]{2,1,0:T(8,128)S(1)}, f32[3,16,8]{2,1,0:T(8,128)S(1)}, u32[]{:S(2)}, u32[]{:S(2)}) collective-permute-start(f32[3,16,8]{2,1,0:T(8,128)S(1)} %get-tuple-element.33), channel_id=1, source_target_pairs={{0,1},{1,2},{2,3},{3,4},{4,5},{5,6},{6,7},{7,8},{8,9},{9,10},{10,1... | collective-permute-start | bytes 4616 | tf_op jit(solution)/shard_map/ppermute | solution.py:75
  40.5 6.0 %collective-permute-start.1 = (f32[3,16,8]{2,1,0:T(8,128)S(1)}, f32[3,16,8]{2,1,0:T(8,128)S(1)}, u32[]{:S(2)}, u32[]{:S(2)}) collective-permute-start(f32[3,16,8]{2,1,0:T(8,128)S(1)} %get-tuple-element.34), channel_id=1, source_target_pairs={{1,0},{2,1},{3,2},{4,3},{5,4},{6,5},{7,6},{8,7},{9,8},{10,9},{11,1... | collective-permute-start | bytes 4616 | tf_op jit(solution)/shard_map/ppermute | solution.py:76
  47.7 0.7 copy-start.14
  47.7 0.7 copy-start.15
  53.4 6.0 %collective-permute-start.2 = (f32[3,16,8]{2,1,0:T(8,128)S(1)}, f32[3,16,8]{2,1,0:T(8,128)S(1)}, u32[]{:S(2)}, u32[]{:S(2)}) collective-permute-start(f32[3,16,8]{2,1,0:T(8,128)S(1)} %get-tuple-element.31), channel_id=1, source_target_pairs={{0,1},{1,2},{2,3},{3,4},{4,5},{5,6},{6,7},{7,8},{8,9},{9,10},{10,1... | collective-permute-start | bytes 4616 | tf_op jit(solution)/shard_map/ppermute | solution.py:75
  53.4 6.0 %collective-permute-start.3 = (f32[3,16,8]{2,1,0:T(8,128)S(1)}, f32[3,16,8]{2,1,0:T(8,128)S(1)}, u32[]{:S(2)}, u32[]{:S(2)}) collective-permute-start(f32[3,16,8]{2,1,0:T(8,128)S(1)} %get-tuple-element.32), channel_id=1, source_target_pairs={{1,0},{2,1},{3,2},{4,3},{5,4},{6,5},{7,6},{8,7},{9,8},{10,9},{11,1... | collective-permute-start | bytes 4616 | tf_op jit(solution)/shard_map/ppermute | solution.py:76
  74.4 1.0 %copy-start.5 = (f32[2,256,128,1]{2,1,3,0:T(8,128)S(1)}, f32[2,256,128,1]{2,1,3,0:T(8,128)}, u32[]{:S(2)}) copy-start(f32[2,256,128,1]{2,1,3,0:T(8,128)} %constant.119) | copy-start | bytes 786436
  77.0 11.5 %copy-start.4 = (f32[10,16,256]{2,1,0:T(8,128)S(1)}, f32[10,16,256]{2,1,0:T(8,128)}, u32[]{:S(2)}) copy-start(f32[10,16,256]{2,1,0:T(8,128)} %param.21) | copy-start | bytes 491524
  77.0 11.5 %all-to-all-start.3 = ((bf16[16,10,256]{2,1,0:T(8,128)(2,1)}), bf16[16,10,256]{2,1,0:T(8,128)(2,1)S(1)}, u32[]{:S(2)}, u32[]{:S(2)}) async-start(bf16[16,10,256]{2,1,0:T(8,128)(2,1)} %convert_element_type.96), calls=%async_computation.3 | async-start | bytes 262144 | tf_op jit(solution)/shard_map/all_to_all | solution.py:101
